TPU v7x, 128 devices: a whole 4x4x4 slice. The times are simulated.
128 devices in a mesh: book: 8 (over y, core), path: 16 (over z, x).
Axes of the slice: x: 4, y: 4, z: 4, core: 2. Of those that a mesh axis runs over, the one named last changes fastest.
Arguments:
- states: float32 [10, 20, 262144], P(None, None, ('book', 'path')), parts along dimension 2, may hold values from -7.5 to 7.5
- itm_flags: int32 [10, 262144], P(None, ('book', 'path')), parts along dimension 1, may hold values 0 or 1
- terminal: float32 [262144], P(('book', 'path')), parts along dimension 0, may hold values from -3.5 to 5.5
- strike: float32 [8], P('book'), parts along dimension 0, may hold values from 0.025 to 0.035
- date_index: int32 [262144], P(('book', 'path')), parts along dimension 0, may hold values from 0 to 9
Outputs:
- cash_flow: float32 [262144], P(('book', 'path')), parts along dimension 0
- book_price: float32 [8], P('book'), parts along dimension 0
- coefficients: float32 [80, 231], P('book'), parts along dimension 0
There are 8 independent parts, one for each index of `book`. A program takes and returns all parts, laid end to end along the dimension named above; each array names one. Nothing has to cross between parts.
All inputs are finite; a program needn't handle non-finite values. No bound on the sum of `itm_flags` on one device may be relied on, other than what follows from the above.
Results may differ from a plain program's by a relative error of at most 0.0003.
Values sent between devices are 32-bit elements; how exact they have to be, the bound alone decides.
A program may use at most 192 MiB of HBM per device.

v0:
```python
import jax
import jax.numpy as jnp
import numpy as np
from jax import lax
from jax.sharding import Mesh
from jax.sharding import PartitionSpec as P

PATH = ("path_0", "path_1")
BOOK_PATH = ("book", "path_0", "path_1")
ridge_weight = 0.05
temper_scale = 0.5
highest = lax.Precision.HIGHEST


def one_axis_at_a_time(shard, axes):
    for axis in axes:
        shard = lax.psum(shard, axis)
    return shard


def sent_to_all(shard, axis):
    length = lax.axis_size(axis)
    return lax.all_to_all(
        jnp.broadcast_to(shard[None], (length, *shard.shape)), axis, 0, 0, tiled=True
    )


def over_copies(shard, axis):
    return sent_to_all(shard, axis).sum(axis=0)


def swap_terms(factors, strike_level):
    forwards = 0.03 * jnp.exp(0.25 * factors)
    discount = jnp.cumprod(1.0 / (1.0 + 0.25 * forwards), axis=0)
    annuity = 0.25 * jnp.sum(discount, axis=0)
    swap_rate = (1.0 - discount[-1]) / annuity
    return (100.0 * annuity * (swap_rate - strike_level), discount[0])


def basis_of(scaled, pair_left, pair_right):
    ones_row = jnp.ones((1, scaled.shape[1]), jnp.float32)
    return jnp.concatenate([ones_row, scaled, scaled[pair_left] * scaled[pair_right]], axis=0)


def gram_only(basis_rows, money_flags):
    weighted = basis_rows * money_flags
    return lax.dot_general(
        weighted,
        basis_rows,
        (((1,), (1,)), ((), ())),
        precision=highest,
        preferred_element_type=jnp.float32,
    )


def system_of(gram_sums, path_count):
    return gram_sums / path_count + ridge_weight * jnp.eye(gram_sums.shape[0], dtype=jnp.float32)


def shards(states, itm_flags, terminal, strike, date_index):
    date_count, factor_count, local_paths = states.shape
    pair_left, pair_right = np.triu_indices(factor_count)
    total_paths = local_paths * lax.axis_size(PATH)
    value_now = terminal
    coef_list = []
    money_all = itm_flags.astype(jnp.float32)
    count_all, first_all, second_all = (
        one_axis_at_a_time(jnp.sum(money_all, axis=1), PATH),
        one_axis_at_a_time(jnp.sum(money_all[:, None, :] * states, axis=2), PATH),
        one_axis_at_a_time(jnp.sum(money_all[:, None, :] * states * states, axis=2), PATH),
    )
    mean_all = first_all / count_all[:, None]
    scale_all = jnp.sqrt(second_all / count_all[:, None] - mean_all * mean_all + 1e-05)
    local_list = []
    for date_step in range(date_count):
        scaled = (states[date_step] - mean_all[date_step][:, None]) / scale_all[date_step][:, None]
        local_list.append(gram_only(basis_of(scaled, pair_left, pair_right), money_all[date_step]))
    gram_stack = lax.psum(jnp.stack(local_list, axis=0), PATH)
    chol_list = [
        jnp.linalg.cholesky(system_of(gram_stack[date_step], count_all[date_step]))
        for date_step in range(date_count)
    ]
    for date_step in range(date_count - 1, -1, -1):
        factors = states[date_step]
        exercise, discount = swap_terms(factors, strike[0])
        value_now = value_now * discount
        money_flags = money_all[date_step]
        scaled = (factors - mean_all[date_step][:, None]) / scale_all[date_step][:, None]
        basis_rows = basis_of(scaled, pair_left, pair_right)
        rhs_local = jnp.dot(
            basis_rows * money_flags,
            value_now,
            precision=highest,
            preferred_element_type=jnp.float32,
        )
        rhs_total = over_copies(rhs_local, PATH)
        coef_vector = jax.scipy.linalg.cho_solve(
            (chol_list[date_step], True), rhs_total / count_all[date_step]
        )
        continuation = jnp.dot(
            coef_vector, basis_rows, precision=highest, preferred_element_type=jnp.float32
        )
        open_date = (date_index <= date_step).astype(jnp.float32)
        weights = jax.nn.sigmoid((exercise - continuation) / temper_scale) * money_flags * open_date
        value_now = value_now + weights * (exercise - value_now)
        coef_list.append(coef_vector)
    book_sum = one_axis_at_a_time(jnp.sum(value_now), PATH)
    book_price = jnp.reshape(book_sum / total_paths, (1,))
    return (value_now, book_price, jnp.stack(coef_list[::-1], axis=0))


def solution(mesh):
    split = Mesh(mesh.devices.reshape(mesh.shape["book"], 4, 4), ("book", "path_0", "path_1"))
    return jax.shard_map(
        shards,
        mesh=split,
        in_specs=(
            P(None, None, BOOK_PATH),
            P(None, BOOK_PATH),
            P(BOOK_PATH),
            P("book"),
            P(BOOK_PATH),
        ),
        out_specs=(P(BOOK_PATH), P("book"), P("book", None)),
        check_vma=False,
    )
```

profile of v0, /device:TPU:0, one launch (start us, length us, event | category | flops | bytes accessed | tf_op | source)
XLA Modules:
  0.0 1114.3 jit_solution(1723377565558352581)
XLA Ops:
  11.3 18.4 %all-reduce.4 = (f32[10,20]{1,0:T(8,128)S(1)}, f32[10]{0:T(128)S(1)}, f32[10,20]{1,0:T(8,128)S(1)}) all-reduce(f32[10,20]{1,0:T(8,128)S(1)} %get-tuple-element.80, f32[10]{0:T(128)S(1)} %convert_reduce_fusion, f32[10,20]{1,0:T(8,128)S(1)} %get-tuple-element.79), channel_id=1, replica_groups=mesh['book'=8,'path_0'=4,'path_1'=4] {'path_0'}, use_global_device_ids=true, to_apply=%region_9.0 | all-reduce | flops 410 | bytes 3280 | tf_op jit(solution)/shard_map/psum | solution.py:17
  29.7 17.0 %all-reduce.3 = (f32[10,20]{1,0:T(8,128)S(1)}, f32[10]{0:T(128)S(1)}, f32[10,20]{1,0:T(8,128)S(1)}) all-reduce(f32[10,20]{1,0:T(8,128)S(1)} %get-tuple-element.84, f32[10]{0:T(128)S(1)} %get-tuple-element.85, f32[10,20]{1,0:T(8,128)S(1)} %get-tuple-element.86), channel_id=1, replica_groups=mesh['book'=8,'path_0'=4,'path_1'=4] {'path_1'}, use_global_device_ids=true, to_apply=%region_10.11 | all-reduce | flops 410 | bytes 3280 | tf_op jit(solution)/shard_map/psum | solution.py:17
  184.8 69.2 %all-reduce.7.cloned.1.call-done = f32[10,231,231]{1,2,0:T(8,128)} async-done(((f32[10,231,231]{1,2,0:T(8,128)}), f32[10,231,231]{1,2,0:T(8,128)}) %all-reduce.7.cloned.1.call-update) | async-done | bytes 2134456 | tf_op jit(solution)/shard_map/psum | solution.py:78
  257.5 11.7 %cholesky.504 = f32[128,128]{1,0:T(8,128)S(1)} custom-call(f32[128,128]{1,0:T(8,128)S(1)} %cholesky.880), custom_call_target="Cholesky" | custom-call | tf_op jit(solution)/shard_map/jit(cholesky)/cholesky | solution.py:80
  304.6 12.1 %cholesky.846 = f32[128,128]{1,0:T(8,128)S(1)} custom-call(f32[128,128]{1,0:T(8,128)S(1)} %cholesky.907), custom_call_target="Cholesky" | custom-call | tf_op jit(solution)/shard_map/jit(cholesky)/cholesky | solution.py:80
  348.6 12.7 %cholesky.808 = f32[128,128]{1,0:T(8,128)S(1)} custom-call(f32[128,128]{1,0:T(8,128)} %cholesky.904), custom_call_target="Cholesky" | custom-call | tf_op jit(solution)/shard_map/jit(cholesky)/cholesky | solution.py:80
  363.2 10.6 custom-call.47
  396.5 12.5 %cholesky.770 = f32[128,128]{1,0:T(8,128)S(1)} custom-call(f32[128,128]{1,0:T(8,128)} %cholesky.901), custom_call_target="Cholesky" | custom-call | tf_op jit(solution)/shard_map/jit(cholesky)/cholesky | solution.py:80
  442.9 11.7 %cholesky.732 = f32[128,128]{1,0:T(8,128)S(1)} custom-call(f32[128,128]{1,0:T(8,128)S(1)} %cholesky.898), custom_call_target="Cholesky" | custom-call | tf_op jit(solution)/shard_map/jit(cholesky)/cholesky | solution.py:80
  484.1 11.7 %cholesky.694 = f32[128,128]{1,0:T(8,128)S(1)} custom-call(f32[128,128]{1,0:T(8,128)S(1)} %cholesky.895), custom_call_target="Cholesky" | custom-call | tf_op jit(solution)/shard_map/jit(cholesky)/cholesky | solution.py:80
  523.6 11.9 %cholesky.656 = f32[128,128]{1,0:T(8,128)S(1)} custom-call(f32[128,128]{1,0:T(8,128)S(1)} %cholesky.892), custom_call_target="Cholesky" | custom-call | tf_op jit(solution)/shard_map/jit(cholesky)/cholesky | solution.py:80
  561.8 11.7 %cholesky.618 = f32[128,128]{1,0:T(8,128)S(1)} custom-call(f32[128,128]{1,0:T(8,128)S(1)} %cholesky.889), custom_call_target="Cholesky" | custom-call | tf_op jit(solution)/shard_map/jit(cholesky)/cholesky | solution.py:80
  600.0 11.7 %cholesky.580 = f32[128,128]{1,0:T(8,128)S(1)} custom-call(f32[128,128]{1,0:T(8,128)S(1)} %cholesky.886), custom_call_target="Cholesky" | custom-call | tf_op jit(solution)/shard_map/jit(cholesky)/cholesky | solution.py:80
  638.1 11.7 %cholesky.542 = f32[128,128]{1,0:T(8,128)S(1)} custom-call(f32[128,128]{1,0:T(8,128)S(1)} %cholesky.883), custom_call_target="Cholesky" | custom-call | tf_op jit(solution)/shard_map/jit(cholesky)/cholesky | solution.py:80
  676.6 19.7 %custom-call.32 = f32[2,128,128]{1,2,0:T(8,128)S(1)} custom-call(f32[2,128,128]{2,1,0:T(8,128)S(1)} %pad_maximum_fusion.10), custom_call_target="InvertDiagBlocksLowerTriangular" | custom-call | tf_op jit(solution)/shard_map/jit(_cho_solve)/triangular_solve | solution.py:97
  719.7 21.1 %custom-call.50 = f32[2,128,128]{1,2,0:T(8,128)} custom-call(f32[2,128,128]{2,1,0:T(8,128)} %pad_maximum_fusion.19), custom_call_target="InvertDiagBlocksLowerTriangular" | custom-call | tf_op jit(solution)/shard_map/jit(_cho_solve)/triangular_solve | solution.py:97
  740.8 21.1 %custom-call.36 = f32[2,128,128]{1,2,0:T(8,128)} custom-call(f32[2,128,128]{2,1,0:T(8,128)} %pad_maximum_fusion.12), custom_call_target="InvertDiagBlocksLowerTriangular" | custom-call | tf_op jit(solution)/shard_map/jit(_cho_solve)/triangular_solve | solution.py:97
  761.9 21.1 %custom-call.38 = f32[2,128,128]{1,2,0:T(8,128)} custom-call(f32[2,128,128]{2,1,0:T(8,128)} %pad_maximum_fusion.13), custom_call_target="InvertDiagBlocksLowerTriangular" | custom-call | tf_op jit(solution)/shard_map/jit(_cho_solve)/triangular_solve | solution.py:97
  783.0 21.1 %custom-call.40 = f32[2,128,128]{1,2,0:T(8,128)} custom-call(f32[2,128,128]{2,1,0:T(8,128)} %pad_maximum_fusion.14), custom_call_target="InvertDiagBlocksLowerTriangular" | custom-call | tf_op jit(solution)/shard_map/jit(_cho_solve)/triangular_solve | solution.py:97
  804.1 21.1 %custom-call.42 = f32[2,128,128]{1,2,0:T(8,128)} custom-call(f32[2,128,128]{2,1,0:T(8,128)} %pad_maximum_fusion.15), custom_call_target="InvertDiagBlocksLowerTriangular" | custom-call | tf_op jit(solution)/shard_map/jit(_cho_solve)/triangular_solve | solution.py:97
  825.2 21.3 %custom-call.44 = f32[2,128,128]{1,2,0:T(8,128)} custom-call(f32[2,128,128]{2,1,0:T(8,128)} %pad_maximum_fusion.16), custom_call_target="InvertDiagBlocksLowerTriangular" | custom-call | tf_op jit(solution)/shard_map/jit(_cho_solve)/triangular_solve | solution.py:97
  846.5 21.1 %custom-call.46 = f32[2,128,128]{1,2,0:T(8,128)} custom-call(f32[2,128,128]{2,1,0:T(8,128)} %pad_maximum_fusion.17), custom_call_target="InvertDiagBlocksLowerTriangular" | custom-call | tf_op jit(solution)/shard_map/jit(_cho_solve)/triangular_solve | solution.py:97
  867.6 21.1 %custom-call.48 = f32[2,128,128]{1,2,0:T(8,128)} custom-call(f32[2,128,128]{2,1,0:T(8,128)} %pad_maximum_fusion.18), custom_call_target="InvertDiagBlocksLowerTriangular" | custom-call | tf_op jit(solution)/shard_map/jit(_cho_solve)/triangular_solve | solution.py:97
  888.7 21.1 %custom-call.34 = f32[2,128,128]{1,2,0:T(8,128)} custom-call(f32[2,128,128]{2,1,0:T(8,128)} %pad_maximum_fusion.11), custom_call_target="InvertDiagBlocksLowerTriangular" | custom-call | tf_op jit(solution)/shard_map/jit(_cho_solve)/triangular_solve | solution.py:97
  (692 shorter events, 637.9 us)
Async XLA Ops:
  9.2 117.4 %copy-start.71 = (f32[1,2048]{1,0:T(1,128)}, f32[1,2048]{1,0:T(1,128)S(1)}, u32[]{:S(2)}) copy-start(f32[1,2048]{1,0:T(1,128)S(1)} %get-tuple-element.145) | copy-start | bytes 24580
  9.2 126.6 %copy-start.75 = (f32[1,2048]{1,0:T(1,128)}, f32[1,2048]{1,0:T(1,128)S(1)}, u32[]{:S(2)}) copy-start(f32[1,2048]{1,0:T(1,128)S(1)} %get-tuple-element.144) | copy-start | bytes 24580
  9.2 129.3 %copy-start.77 = (f32[1,2048]{1,0:T(1,128)}, f32[1,2048]{1,0:T(1,128)S(1)}, u32[]{:S(2)}) copy-start(f32[1,2048]{1,0:T(1,128)S(1)} %get-tuple-element.143) | copy-start | bytes 24580
  9.2 132.0 %copy-start.79 = (f32[1,2048]{1,0:T(1,128)}, f32[1,2048]{1,0:T(1,128)S(1)}, u32[]{:S(2)}) copy-start(f32[1,2048]{1,0:T(1,128)S(1)} %get-tuple-element.142) | copy-start | bytes 24580
  9.3 134.7 %copy-start.81 = (f32[1,2048]{1,0:T(1,128)}, f32[1,2048]{1,0:T(1,128)S(1)}, u32[]{:S(2)}) copy-start(f32[1,2048]{1,0:T(1,128)S(1)} %get-tuple-element.141) | copy-start | bytes 24580
  9.3 137.6 %copy-start.83 = (f32[1,2048]{1,0:T(1,128)}, f32[1,2048]{1,0:T(1,128)S(1)}, u32[]{:S(2)}) copy-start(f32[1,2048]{1,0:T(1,128)S(1)} %get-tuple-element.140) | copy-start | bytes 24580
  9.3 140.3 %copy-start.85 = (f32[1,2048]{1,0:T(1,128)}, f32[1,2048]{1,0:T(1,128)S(1)}, u32[]{:S(2)}) copy-start(f32[1,2048]{1,0:T(1,128)S(1)} %get-tuple-element.139) | copy-start | bytes 24580
  9.3 143.0 %copy-start.88 = (f32[1,2048]{1,0:T(1,128)}, f32[1,2048]{1,0:T(1,128)S(1)}, u32[]{:S(2)}) copy-start(f32[1,2048]{1,0:T(1,128)S(1)} %get-tuple-element.138) | copy-start | bytes 24580
  9.3 145.7 %copy-start.90 = (f32[1,2048]{1,0:T(1,128)}, f32[1,2048]{1,0:T(1,128)S(1)}, u32[]{:S(2)}) copy-start(f32[1,2048]{1,0:T(1,128)S(1)} %get-tuple-element.137) | copy-start | bytes 24580
  9.3 148.4 %copy-start.96 = (f32[1,2048]{1,0:T(1,128)}, f32[1,2048]{1,0:T(1,128)S(1)}, u32[]{:S(2)}) copy-start(f32[1,2048]{1,0:T(1,128)S(1)} %get-tuple-element.146) | copy-start | bytes 24580
  60.6 97.1 %copy-start.127 = (f32[1,2048]{1,0:T(1,128)}, f32[1,2048]{1,0:T(1,128)S(1)}, u32[]{:S(2)}) copy-start(f32[1,2048]{1,0:T(1,128)S(1)} %broadcast.242) | copy-start | bytes 24580
  62.9 121.1 %all-to-all-start = ((f32[16,1,231]{2,1,0:T(1,128)}), f32[16,1,231]{2,1,0:T(1,128)S(1)}, u32[]{:S(2)}, u32[]{:S(2)}) async-start(f32[16,1,231]{2,1,0:T(1,128)} %broadcast_in_dim.208), calls=%async_computation | async-start | bytes 32768 | tf_op jit(solution)/shard_map/all_to_all | solution.py:23
  66.7 187.3 %all-reduce.7.cloned.1.call-start = ((), (), s32[]{:S(2)}) async-start(), calls=%async_computation.10 | async-start | bytes 4751360 | tf_op jit(solution)/shard_map/psum | solution.py:78
  704.3 205.5 %all-to-all-start.1 = ((f32[16,1,231]{2,1,0:T(1,128)}), f32[16,1,231]{2,1,0:T(1,128)}, u32[]{:S(2)}, u32[]{:S(2)}) async-start(f32[16,1,231]{2,1,0:T(1,128)} %broadcast_in_dim.211), calls=%async_computation.1 | async-start | bytes 32768 | tf_op jit(solution)/shard_map/all_to_all | solution.py:23
  713.0 208.9 %copy-start.31 = (f32[210,2048]{1,0:T(8,128)S(1)}, f32[210,2048]{1,0:T(8,128)}, u32[]{:S(2)}) copy-start(f32[210,2048]{1,0:T(8,128)} %copy-done.30) | copy-start | bytes 5160964
  713.0 208.9 %copy-start.89 = (f32[1,2048]{1,0:T(1,128)S(1)}, f32[1,2048]{1,0:T(1,128)}, u32[]{:S(2)}) copy-start(f32[1,2048]{1,0:T(1,128)} %copy-done.88) | copy-start | bytes 24580
  924.3 14.9 %all-to-all-start.2 = ((f32[16,1,231]{2,1,0:T(1,128)}), f32[16,1,231]{2,1,0:T(1,128)S(1)}, u32[]{:S(2)}, u32[]{:S(2)}) async-start(f32[16,1,231]{2,1,0:T(1,128)} %broadcast_in_dim.214), calls=%async_computation.2 | async-start | bytes 32768 | tf_op jit(solution)/shard_map/all_to_all | solution.py:23
  951.0 11.0 all-to-all-start.3
  970.4 11.0 all-to-all-start.4
  990.0 11.4 %all-to-all-start.5 = ((f32[16,1,231]{2,1,0:T(1,128)}), f32[16,1,231]{2,1,0:T(1,128)S(1)}, u32[]{:S(2)}, u32[]{:S(2)}) async-start(f32[16,1,231]{2,1,0:T(1,128)} %broadcast_in_dim.223), calls=%async_computation.5 | async-start | bytes 32768 | tf_op jit(solution)/shard_map/all_to_all | solution.py:23
  1009.8 11.0 all-to-all-start.6
  1029.3 11.0 all-to-all-start.7
  1048.7 11.2 %all-to-all-start.8 = ((f32[16,1,231]{2,1,0:T(1,128)}), f32[16,1,231]{2,1,0:T(1,128)S(1)}, u32[]{:S(2)}, u32[]{:S(2)}) async-start(f32[16,1,231]{2,1,0:T(1,128)} %broadcast_in_dim.232), calls=%async_computation.8 | async-start | bytes 32768 | tf_op jit(solution)/shard_map/all_to_all | solution.py:23
  1068.4 11.0 all-to-all-start.9
  (131 other events, 1780.0 us)
Sparse Core Ops, SparseCore 0:
  160.6 93.2 all-reduce.6
where the time goes:
time: 1120 us; the launch traced here: 1110 us
  other arithmetic  630 us (56%)
  waiting for transfers between devices  127 us (11%)
  matrix products  123 us (11%)
  local copies, waits for them, and re-layouts  106 us (9%)
  blocking collectives  54.3 us (5%)
  starting transfers between devices  41.8 us (4%)
  between operations  31.9 us (3%)
    another operation x70, other arithmetic, shards(): jnp.linalg.cholesky(system_of(gram_stack[date_step], count_all[date_step]))  336 us
    another operation x34, other arithmetic, shards(): jax.scipy.linalg.cho_solve((chol_list[date_step], True), rhs_total / coun...  229 us
    psum x1, waiting for transfers between devices, shards(): gram_stack = lax.psum(jnp.stack(local_list, axis=0), PATH)  69.2 us
    all_to_all x10, waiting for transfers between devices, sent_to_all(): lax.all_to_all(jnp.broadcast_to(shard[None], (length, *shard.shape)), axi...  58 us
    psum x4, blocking collectives, one_axis_at_a_time(): shard = lax.psum(shard, axis)  54.3 us
    all_to_all x10, starting transfers between devices, sent_to_all(): lax.all_to_all(jnp.broadcast_to(shard[None], (length, *shard.shape)), axi...  41.5 us
    another operation x60, matrix products, shards(): jax.scipy.linalg.cho_solve((chol_list[date_step], True), rhs_total / coun...  33.7 us
    dot_general x10, matrix products, gram_only(): lax.dot_general(weighted, basis_rows, (((1,), (1,)), ((), ())), precision...  27.3 us
  transfers between devices with their start and end apart: 11, of which 9 were waited for; matrix products, arithmetic and copies ran while one was open for 27% of the time, Pallas kernels for 0%

commit v1 on v0

--- a/solution.py
+++ b/solution.py
@@ -75,7 +75,10 @@
     for date_step in range(date_count):
         scaled = (states[date_step] - mean_all[date_step][:, None]) / scale_all[date_step][:, None]
         local_list.append(gram_only(basis_of(scaled, pair_left, pair_right), money_all[date_step]))
-    gram_stack = lax.psum(jnp.stack(local_list, axis=0), PATH)
+    number_ways = lambda panel, bus_axis, group_axis: jax.lax.psum(
+        jax.lax.psum(panel, axis_name=bus_axis), axis_name=group_axis
+    )
+    gram_stack = number_ways(jnp.stack(local_list, axis=0), "path_1", "path_0")
     chol_list = [
         jnp.linalg.cholesky(system_of(gram_stack[date_step], count_all[date_step]))
         for date_step in range(date_count)

time: 1120 us -> 1180 us (1.054)
  waiting for transfers between devices: 127 us -> 167 us
    psum x1 -> x2, waiting for transfers between devices: 69.2 us -> 107 us  [the longest x1 55.6 us: shards(): jax.lax.psum(panel, axis_name=bus_axis)]
    dot_general x10, matrix products: 16.6 us -> 28.5 us  [shards(): jnp.dot(basis_rows * money_flags, value_now, precision=highest, preferred...]
    unnamed x288 -> x218, local copies, waits for them, and re-layouts: 22.9 us -> 24.1 us
  transfers between devices with their start and end apart: 11 -> 12, of which waited for: 9 -> 10; matrix products, arithmetic and copies ran while one was open for 27% -> 26% of each run, Pallas kernels for 0% -> 0%
where the time goes in v1:
time: 1180 us; the launch traced here: 1170 us
  other arithmetic  629 us (53%)
  waiting for transfers between devices  167 us (14%)
  matrix products  131 us (11%)
  local copies, waits for them, and re-layouts  109 us (9%)
  blocking collectives  54.3 us (5%)
  starting transfers between devices  42.6 us (4%)
  between operations  31.5 us (3%)
    another operation x70, other arithmetic, shards(): jnp.linalg.cholesky(system_of(gram_stack[date_step], count_all[date_step]))  336 us
    another operation x34, other arithmetic, shards(): jax.scipy.linalg.cho_solve((chol_list[date_step], True), rhs_total / coun...  231 us
    all_to_all x10, waiting for transfers between devices, sent_to_all(): lax.all_to_all(jnp.broadcast_to(shard[None], (length, *shard.shape)), axi...  60.1 us
    psum x1, waiting for transfers between devices, shards(): jax.lax.psum(panel, axis_name=bus_axis)  55.6 us
    psum x4, blocking collectives, one_axis_at_a_time(): shard = lax.psum(shard, axis)  54.3 us
    psum x1, waiting for transfers between devices, shards(): jax.lax.psum(jax.lax.psum(panel, axis_name=bus_axis), axis_name=group_axis)  51.5 us
    all_to_all x10, starting transfers between devices, sent_to_all(): lax.all_to_all(jnp.broadcast_to(shard[None], (length, *shard.shape)), axi...  42 us
    dot_general x10, matrix products, shards(): jnp.dot(basis_rows * money_flags, value_now, precision=highest, preferred...  28.5 us
  transfers between devices with their start and end apart: 12, of which 10 were waited for; matrix products, arithmetic and copies ran while one was open for 26% of the time, Pallas kernels for 0%

profile of v1, /device:TPU:0, one launch (start us, length us, event | category | flops | bytes accessed | tf_op | source)
XLA Modules:
  0.0 1165.6 jit_solution(16037307403477612320)
XLA Ops:
  11.3 18.4 %all-reduce.4 = (f32[10,20]{1,0:T(8,128)S(1)}, f32[10]{0:T(128)S(1)}, f32[10,20]{1,0:T(8,128)S(1)}) all-reduce(f32[10,20]{1,0:T(8,128)S(1)} %get-tuple-element.80, f32[10]{0:T(128)S(1)} %convert_reduce_fusion, f32[10,20]{1,0:T(8,128)S(1)} %get-tuple-element.79), channel_id=1, replica_groups=mesh['book'=8,'path_0'=4,'path_1'=4] {'path_0'}, use_global_device_ids=true, to_apply=%region_9.0 | all-reduce | flops 410 | bytes 3280 | tf_op jit(solution)/shard_map/psum | solution.py:17
  29.7 17.0 %all-reduce.3 = (f32[10,20]{1,0:T(8,128)S(1)}, f32[10]{0:T(128)S(1)}, f32[10,20]{1,0:T(8,128)S(1)}) all-reduce(f32[10,20]{1,0:T(8,128)S(1)} %get-tuple-element.84, f32[10]{0:T(128)S(1)} %get-tuple-element.85, f32[10,20]{1,0:T(8,128)S(1)} %get-tuple-element.86), channel_id=1, replica_groups=mesh['book'=8,'path_0'=4,'path_1'=4] {'path_1'}, use_global_device_ids=true, to_apply=%region_10.0 | all-reduce | flops 410 | bytes 3280 | tf_op jit(solution)/shard_map/psum | solution.py:17
  170.0 55.6 %all-reduce.8.cloned.1.call-done = f32[10,231,231]{1,2,0:T(8,128)} async-done(((f32[10,231,231]{1,2,0:T(8,128)}), f32[10,231,231]{1,2,0:T(8,128)}) %all-reduce.8.cloned.1.call-update) | async-done | bytes 2134456 | tf_op jit(solution)/shard_map/psum | solution.py:79
  239.9 51.5 %all-reduce.10.cloned.1.call-done = f32[10,231,231]{1,2,0:T(8,128)} async-done(((f32[10,231,231]{1,2,0:T(8,128)}), f32[10,231,231]{1,2,0:T(8,128)}) %all-reduce.10.cloned.1.call-update) | async-done | bytes 2134456 | tf_op jit(solution)/shard_map/psum | solution.py:78
  294.8 11.7 %cholesky.504 = f32[128,128]{1,0:T(8,128)S(1)} custom-call(f32[128,128]{1,0:T(8,128)S(1)} %cholesky.880), custom_call_target="Cholesky" | custom-call | tf_op jit(solution)/shard_map/jit(cholesky)/cholesky | solution.py:83
  342.2 12.1 %cholesky.846 = f32[128,128]{1,0:T(8,128)S(1)} custom-call(f32[128,128]{1,0:T(8,128)S(1)} %cholesky.907), custom_call_target="Cholesky" | custom-call | tf_op jit(solution)/shard_map/jit(cholesky)/cholesky | solution.py:83
  386.1 12.7 %cholesky.808 = f32[128,128]{1,0:T(8,128)S(1)} custom-call(f32[128,128]{1,0:T(8,128)} %cholesky.904), custom_call_target="Cholesky" | custom-call | tf_op jit(solution)/shard_map/jit(cholesky)/cholesky | solution.py:83
  434.0 12.5 %cholesky.770 = f32[128,128]{1,0:T(8,128)S(1)} custom-call(f32[128,128]{1,0:T(8,128)} %cholesky.901), custom_call_target="Cholesky" | custom-call | tf_op jit(solution)/shard_map/jit(cholesky)/cholesky | solution.py:83
  480.3 11.7 %cholesky.732 = f32[128,128]{1,0:T(8,128)S(1)} custom-call(f32[128,128]{1,0:T(8,128)S(1)} %cholesky.898), custom_call_target="Cholesky" | custom-call | tf_op jit(solution)/shard_map/jit(cholesky)/cholesky | solution.py:83
  521.5 11.7 %cholesky.694 = f32[128,128]{1,0:T(8,128)S(1)} custom-call(f32[128,128]{1,0:T(8,128)S(1)} %cholesky.895), custom_call_target="Cholesky" | custom-call | tf_op jit(solution)/shard_map/jit(cholesky)/cholesky | solution.py:83
  562.2 11.9 %cholesky.656 = f32[128,128]{1,0:T(8,128)S(1)} custom-call(f32[128,128]{1,0:T(8,128)S(1)} %cholesky.892), custom_call_target="Cholesky" | custom-call | tf_op jit(solution)/shard_map/jit(cholesky)/cholesky | solution.py:83
  603.1 11.7 %cholesky.618 = f32[128,128]{1,0:T(8,128)S(1)} custom-call(f32[128,128]{1,0:T(8,128)S(1)} %cholesky.889), custom_call_target="Cholesky" | custom-call | tf_op jit(solution)/shard_map/jit(cholesky)/cholesky | solution.py:83
  644.2 11.7 %cholesky.580 = f32[128,128]{1,0:T(8,128)S(1)} custom-call(f32[128,128]{1,0:T(8,128)S(1)} %cholesky.886), custom_call_target="Cholesky" | custom-call | tf_op jit(solution)/shard_map/jit(cholesky)/cholesky | solution.py:83
  685.1 11.7 %cholesky.542 = f32[128,128]{1,0:T(8,128)S(1)} custom-call(f32[128,128]{1,0:T(8,128)S(1)} %cholesky.883), custom_call_target="Cholesky" | custom-call | tf_op jit(solution)/shard_map/jit(cholesky)/cholesky | solution.py:83
  726.6 20.5 %custom-call.32 = f32[2,128,128]{1,2,0:T(8,128)S(1)} custom-call(f32[2,128,128]{2,1,0:T(8,128)} %pad_maximum_fusion.10), custom_call_target="InvertDiagBlocksLowerTriangular" | custom-call | tf_op jit(solution)/shard_map/jit(_cho_solve)/triangular_solve | solution.py:100
  774.6 20.5 %custom-call.50 = f32[2,128,128]{1,2,0:T(8,128)S(1)} custom-call(f32[2,128,128]{2,1,0:T(8,128)} %pad_maximum_fusion.19), custom_call_target="InvertDiagBlocksLowerTriangular" | custom-call | tf_op jit(solution)/shard_map/jit(_cho_solve)/triangular_solve | solution.py:100
  795.1 20.3 %custom-call.36 = f32[2,128,128]{1,2,0:T(8,128)} custom-call(f32[2,128,128]{2,1,0:T(8,128)S(1)} %pad_maximum_fusion.12), custom_call_target="InvertDiagBlocksLowerTriangular" | custom-call | tf_op jit(solution)/shard_map/jit(_cho_solve)/triangular_solve | solution.py:100
  815.4 21.1 %custom-call.38 = f32[2,128,128]{1,2,0:T(8,128)} custom-call(f32[2,128,128]{2,1,0:T(8,128)} %pad_maximum_fusion.13), custom_call_target="InvertDiagBlocksLowerTriangular" | custom-call | tf_op jit(solution)/shard_map/jit(_cho_solve)/triangular_solve | solution.py:100
  836.5 21.1 %custom-call.40 = f32[2,128,128]{1,2,0:T(8,128)} custom-call(f32[2,128,128]{2,1,0:T(8,128)} %pad_maximum_fusion.14), custom_call_target="InvertDiagBlocksLowerTriangular" | custom-call | tf_op jit(solution)/shard_map/jit(_cho_solve)/triangular_solve | solution.py:100
  857.5 21.1 %custom-call.42 = f32[2,128,128]{1,2,0:T(8,128)} custom-call(f32[2,128,128]{2,1,0:T(8,128)} %pad_maximum_fusion.15), custom_call_target="InvertDiagBlocksLowerTriangular" | custom-call | tf_op jit(solution)/shard_map/jit(_cho_solve)/triangular_solve | solution.py:100
  878.6 20.4 %custom-call.44 = f32[2,128,128]{1,2,0:T(8,128)} custom-call(f32[2,128,128]{2,1,0:T(8,128)S(1)} %pad_maximum_fusion.16), custom_call_target="InvertDiagBlocksLowerTriangular" | custom-call | tf_op jit(solution)/shard_map/jit(_cho_solve)/triangular_solve | solution.py:100
  899.1 20.5 %custom-call.46 = f32[2,128,128]{1,2,0:T(8,128)S(1)} custom-call(f32[2,128,128]{2,1,0:T(8,128)} %pad_maximum_fusion.17), custom_call_target="InvertDiagBlocksLowerTriangular" | custom-call | tf_op jit(solution)/shard_map/jit(_cho_solve)/triangular_solve | solution.py:100
  919.6 20.5 %custom-call.48 = f32[2,128,128]{1,2,0:T(8,128)S(1)} custom-call(f32[2,128,128]{2,1,0:T(8,128)} %pad_maximum_fusion.18), custom_call_target="InvertDiagBlocksLowerTriangular" | custom-call | tf_op jit(solution)/shard_map/jit(_cho_solve)/triangular_solve | solution.py:100
  940.0 21.1 %custom-call.34 = f32[2,128,128]{1,2,0:T(8,128)} custom-call(f32[2,128,128]{2,1,0:T(8,128)} %pad_maximum_fusion.11), custom_call_target="InvertDiagBlocksLowerTriangular" | custom-call | tf_op jit(solution)/shard_map/jit(_cho_solve)/triangular_solve | solution.py:100
  (625 shorter events, 665.2 us)
Async XLA Ops:
  9.2 126.5 %copy-start.55 = (f32[1,2048]{1,0:T(1,128)}, f32[1,2048]{1,0:T(1,128)S(1)}, u32[]{:S(2)}) copy-start(f32[1,2048]{1,0:T(1,128)S(1)} %get-tuple-element.144) | copy-start | bytes 24580
  9.2 129.3 %copy-start.57 = (f32[1,2048]{1,0:T(1,128)}, f32[1,2048]{1,0:T(1,128)S(1)}, u32[]{:S(2)}) copy-start(f32[1,2048]{1,0:T(1,128)S(1)} %get-tuple-element.143) | copy-start | bytes 24580
  9.2 132.0 %copy-start.59 = (f32[1,2048]{1,0:T(1,128)}, f32[1,2048]{1,0:T(1,128)S(1)}, u32[]{:S(2)}) copy-start(f32[1,2048]{1,0:T(1,128)S(1)} %get-tuple-element.142) | copy-start | bytes 24580
  9.3 134.7 %copy-start.61 = (f32[1,2048]{1,0:T(1,128)}, f32[1,2048]{1,0:T(1,128)S(1)}, u32[]{:S(2)}) copy-start(f32[1,2048]{1,0:T(1,128)S(1)} %get-tuple-element.141) | copy-start | bytes 24580
  9.3 137.6 %copy-start.63 = (f32[1,2048]{1,0:T(1,128)}, f32[1,2048]{1,0:T(1,128)S(1)}, u32[]{:S(2)}) copy-start(f32[1,2048]{1,0:T(1,128)S(1)} %get-tuple-element.140) | copy-start | bytes 24580
  9.3 140.3 %copy-start.65 = (f32[1,2048]{1,0:T(1,128)}, f32[1,2048]{1,0:T(1,128)S(1)}, u32[]{:S(2)}) copy-start(f32[1,2048]{1,0:T(1,128)S(1)} %get-tuple-element.139) | copy-start | bytes 24580
  9.3 143.0 %copy-start.67 = (f32[1,2048]{1,0:T(1,128)}, f32[1,2048]{1,0:T(1,128)S(1)}, u32[]{:S(2)}) copy-start(f32[1,2048]{1,0:T(1,128)S(1)} %get-tuple-element.138) | copy-start | bytes 24580
  9.3 145.7 %copy-start.70 = (f32[1,2048]{1,0:T(1,128)}, f32[1,2048]{1,0:T(1,128)S(1)}, u32[]{:S(2)}) copy-start(f32[1,2048]{1,0:T(1,128)S(1)} %get-tuple-element.137) | copy-start | bytes 24580
  9.3 148.4 %copy-start.74 = (f32[1,2048]{1,0:T(1,128)}, f32[1,2048]{1,0:T(1,128)S(1)}, u32[]{:S(2)}) copy-start(f32[1,2048]{1,0:T(1,128)S(1)} %get-tuple-element.146) | copy-start | bytes 24580
  62.9 176.2 %all-to-all-start = ((f32[16,1,231]{2,1,0:T(1,128)}), f32[16,1,231]{2,1,0:T(1,128)S(1)}, u32[]{:S(2)}, u32[]{:S(2)}) async-start(f32[16,1,231]{2,1,0:T(1,128)} %broadcast_in_dim.208), calls=%async_computation | async-start | bytes 32768 | tf_op jit(solution)/shard_map/all_to_all | solution.py:23
  66.7 158.9 %all-reduce.8.cloned.1.call-start = ((), (), s32[]{:S(2)}) async-start(), calls=%async_computation.10 | async-start | bytes 4751360 | tf_op jit(solution)/shard_map/psum | solution.py:79
  160.5 130.9 %all-reduce.10.cloned.1.call-start = ((), (), s32[]{:S(2)}) async-start(), calls=%async_computation.11 | async-start | bytes 4751360 | tf_op jit(solution)/shard_map/psum | solution.py:78
  755.0 206.1 %all-to-all-start.1 = ((f32[16,1,231]{2,1,0:T(1,128)}), f32[16,1,231]{2,1,0:T(1,128)S(1)}, u32[]{:S(2)}, u32[]{:S(2)}) async-start(f32[16,1,231]{2,1,0:T(1,128)} %broadcast_in_dim.211), calls=%async_computation.1 | async-start | bytes 32768 | tf_op jit(solution)/shard_map/all_to_all | solution.py:23
  768.0 201.0 %copy-start.80 = (f32[2048]{0:T(1024)S(1)}, f32[2048]{0:T(1024)}, u32[]{:S(2)}) copy-start(f32[2048]{0:T(1024)} %reduce_sum.221) | copy-start | bytes 24580
  768.0 201.0 %copy-start.97 = (f32[1,2048]{1,0:T(1,128)S(1)}, f32[1,2048]{1,0:T(1,128)}, u32[]{:S(2)}) copy-start(f32[1,2048]{1,0:T(1,128)} %get-tuple-element.132) | copy-start | bytes 24580
  768.0 201.8 %copy-start.68 = (f32[1,2048]{1,0:T(1,128)S(1)}, f32[1,2048]{1,0:T(1,128)}, u32[]{:S(2)}) copy-start(f32[1,2048]{1,0:T(1,128)} %copy-done.67) | copy-start | bytes 24580
  973.6 15.1 %all-to-all-start.2 = ((f32[16,1,231]{2,1,0:T(1,128)}), f32[16,1,231]{2,1,0:T(1,128)S(1)}, u32[]{:S(2)}, u32[]{:S(2)}) async-start(f32[16,1,231]{2,1,0:T(1,128)} %broadcast_in_dim.214), calls=%async_computation.2 | async-start | bytes 32768 | tf_op jit(solution)/shard_map/all_to_all | solution.py:23
  997.0 11.0 all-to-all-start.3
  1016.3 11.0 all-to-all-start.4
  1035.6 11.4 all-to-all-start.5
  1055.3 11.0 all-to-all-start.6
  1076.3 11.0 all-to-all-start.7
  1097.2 11.2 all-to-all-start.8
  1118.3 11.0 all-to-all-start.9
  (97 other events, 1529.8 us)
Sparse Core Ops, SparseCore 0:
  160.6 64.9 all-reduce.7
  228.0 63.3 all-reduce.9
